TPU v7x, 32 devices: a whole 2x2x4 slice. The times are simulated.
32 devices in a mesh: gx: 2 (over x), gy: 4 (over z), gz: 4 (over y, core).
Axes of the slice: x: 2, y: 2, z: 4, core: 2. Of those that a mesh axis runs over, the one named last changes fastest.
Arguments:
- pair_list: int32 [1024, 2], P(('gx', 'gy', 'gz')), may hold values from 0 to 63, all different within a row; in each aligned block of 32 rows (0 to 31, 32 to 63, ...) at most 2 rows name the same one
- rank_bucket: int32 [1024], P(('gx', 'gy', 'gz')), may hold values from 0 to 2
- amplitudes: bfloat16 [1024, 36864], P(('gx', 'gy', 'gz')), may hold values from -0.4375 to 0.4375
- intersects: bfloat16 [1024, 36864], P(('gx', 'gy', 'gz')), may hold values from -0.4375 to 0.4375
- integrals: bfloat16 [1024, 36864], P(('gx', 'gy', 'gz')), may hold values from -6 to 6
- exchange_blocks: bfloat16 [64, 36864], P(('gx', 'gy')), may hold values from -0.4375 to 0.4375
Outputs:
- residuals: bfloat16 [1024, 36864], P(('gx', 'gy', 'gz'))
Inputs may be any that keep to these rules, and one draw needn't show every extreme that they name: `pair_list`: each row names two different occupied orbitals; within the rows of one device no orbital is named more than 2 times, a bound that some block reaches on some devices. `rank_bucket`: bucket b keeps the leading (b + 1) * 64 PNOs.
All inputs are finite; a program needn't handle non-finite values.
Results may differ from a plain program's by a relative error of at most 0.013.
Values may be sent and summed in bfloat16 or wider, within the bound.
A program may use at most 128 MiB of HBM per device.

v0:
```python
import jax
import jax.numpy as jnp
from jax import lax
from jax.sharding import PartitionSpec as P

RSTEP = 64
R = 192


def body(pair_list, rank_bucket, amplitudes, intersects, integrals, exchange_blocks):
    pair_rows = amplitudes.shape[0]
    rank_width = R
    owned_rows = exchange_blocks.shape[0]
    amplitudes = amplitudes.reshape(pair_rows, rank_width, rank_width)
    intersects = intersects.reshape(pair_rows, rank_width, rank_width)
    integrals = integrals.reshape(pair_rows, rank_width, rank_width)
    exchange_blocks = exchange_blocks.reshape(owned_rows, rank_width, rank_width)
    groups_x, groups_y = (lax.axis_size("gx"), lax.axis_size("gy"))
    group_total = groups_x * groups_y
    occupied = owned_rows * group_total
    row_index = lax.broadcasted_iota(jnp.int32, (rank_width, rank_width), 0)
    col_index = lax.broadcasted_iota(jnp.int32, (rank_width, rank_width), 1)
    pair_rank = (rank_bucket + 1) * RSTEP
    inside = (row_index[None] < pair_rank[:, None, None]) & (
        col_index[None] < pair_rank[:, None, None]
    )
    masked = jnp.where(inside, amplitudes, jnp.zeros_like(amplitudes))
    half_projected = jnp.einsum(
        "pab,pbc->pac", intersects, masked, preferred_element_type=jnp.float32
    ).astype(jnp.bfloat16)
    projected = jnp.einsum(
        "pab,pcb->pac", half_projected, intersects, preferred_element_type=jnp.float32
    ).astype(jnp.bfloat16)
    local_term = jnp.einsum("pab,pbc->pac", masked, integrals, preferred_element_type=jnp.float32)
    flat_projected = projected.reshape(pair_rows, rank_width * rank_width)
    end_counts = jnp.sum(
        (pair_list[None] == lax.broadcasted_iota(jnp.int32, (occupied, 1, 1), 0)).astype(jnp.int32),
        axis=2,
    ).astype(jnp.bfloat16)
    partial_sum = lax.psum_scatter(
        jnp.dot(end_counts, flat_projected, preferred_element_type=jnp.float32),
        ("gx", "gy"),
        scatter_dimension=0,
        tiled=True,
    ).reshape(owned_rows, rank_width, rank_width)
    domain = lax.psum(partial_sum, "gz")
    coupled = jnp.einsum(
        "oab,obc->oac",
        domain.astype(jnp.bfloat16),
        exchange_blocks,
        preferred_element_type=jnp.float32,
    ).astype(jnp.bfloat16)
    every_coupled, every_block = (
        lax.all_gather(coupled, ("gx", "gy"), axis=0, tiled=True),
        lax.all_gather(exchange_blocks, ("gx", "gy"), axis=0, tiled=True),
    )
    picked_blocks = every_block[pair_list]
    picked_coupled = every_coupled[pair_list]
    own_term = jnp.einsum(
        "pab,pebc->peac", projected, picked_blocks, preferred_element_type=jnp.float32
    ).astype(jnp.bfloat16)
    answers = (picked_coupled.astype(jnp.float32) - own_term.astype(jnp.float32)).astype(
        jnp.bfloat16
    )
    combined = (answers[:, 0].astype(jnp.float32) + answers[:, 1].astype(jnp.float32)).astype(
        jnp.bfloat16
    )
    half_back = jnp.einsum(
        "pba,pbc->pac", intersects, combined, preferred_element_type=jnp.float32
    ).astype(jnp.bfloat16)
    back_projected = jnp.einsum(
        "pab,pbc->pac", half_back, intersects, preferred_element_type=jnp.float32
    )
    residual_sum = integrals.astype(jnp.float32) + local_term + back_projected
    result = jnp.where(inside, residual_sum, jnp.zeros_like(residual_sum)).astype(jnp.bfloat16)
    return result.reshape(pair_rows, rank_width * rank_width)


def solution(mesh):
    placed = (
        P(("gx", "gy", "gz"), None),
        P(("gx", "gy", "gz")),
        P(("gx", "gy", "gz"), None),
        P(("gx", "gy", "gz"), None),
        P(("gx", "gy", "gz"), None),
        P(("gx", "gy"), None),
    )
    return jax.shard_map(
        body, mesh=mesh, in_specs=placed, out_specs=P(("gx", "gy", "gz"), None), check_vma=False
    )
```

profile of v0, /device:TPU:1, one launch (start us, length us, event | category | flops | bytes accessed | tf_op | source)
XLA Modules:
  0.0 452.9 jit_solution(4188154951140406437)
XLA Ops:
  6.5 0.0 reduce-scatter.2.cloned.1.call-start
  6.5 6.1 %reshape.28 = bf16[32,192,192]{2,1,0:T(8,128)(2,1)} reshape(bf16[32,36864]{1,0:T(8,128)(2,1)} %param.8) | data formatting | bytes 4718592 | tf_op jit(solution)/shard_map/reshape | solution.py:14
  12.7 0.0 copy-start.1
  12.7 5.0 %reshape.29 = bf16[32,192,192]{2,1,0:T(8,128)(2,1)S(1)} reshape(bf16[32,36864]{1,0:T(8,128)(2,1)} %param.9) | data formatting | bytes 4718592 | tf_op jit(solution)/shard_map/reshape | solution.py:15
  17.6 0.0 copy-done.1
  17.7 6.9 %fusion.19 = bf16[32,192,192]{2,1,0:T(8,128)(2,1)} fusion(bf16[32,192,192]{2,1,0:T(8,128)(2,1)S(1)} %reshape.29, bf16[32,192,192]{2,1,0:T(8,128)(2,1)} %reshape.28, s32[32]{0:T(128)S(1)} %add_multiply_fusion), kind=kOutput, calls=%fused_computation.20 | convolution fusion | flops 913047552 | bytes 7078016 | tf_op jit(solution)/shard_map/pab,pcb->pac/dot_general | solution.py:31
  24.5 0.0 copy-start
  24.5 6.2 %reshape.30 = bf16[32,36864]{1,0:T(8,128)(2,1)} reshape(bf16[32,192,192]{2,1,0:T(8,128)(2,1)} %fusion.19) | data formatting | bytes 4718592 | tf_op jit(solution)/shard_map/reshape | solution.py:35
  30.7 0.0 copy-done
  30.7 0.1 convert_reduce_fusion
  30.8 6.7 %fusion.26 = f32[64,36864]{1,0:T(8,128)} fusion(bf16[32,36864]{1,0:T(8,128)(2,1)} %reshape.30, s32[64,32]{0,1:T(8,128)S(1)} %convert_reduce_fusion), kind=kOutput, calls=%fused_computation.25 | convolution fusion | flops 150996992 | bytes 11804672 | tf_op jit(solution)/shard_map/dot_general | solution.py:41
  37.5 0.0 reduce-scatter.2.cloned.1.call-update
  37.5 0.0 all-gather.5.cloned.1.call-start
  37.5 2.9 reshape.32
  40.4 0.0 all-gather.5.cloned.1.call-update
  40.5 0.0 all-gather.3.cloned.1.call-start
  40.5 161.2 %reduce-scatter.2.cloned.1.call-done = f32[8,36864]{1,0:T(8,128)} async-done(((f32[64,36864]{1,0:T(8,128)}), f32[8,36864]{1,0:T(8,128)}) %reduce-scatter.2.cloned.1.call-update) | async-done | bytes 1179664 | tf_op jit(solution)/shard_map/reduce_scatter | solution.py:40
  201.7 3.1 reshape.31
  204.8 35.0 %all-reduce.1 = bf16[8,192,192]{2,1,0:T(8,128)(2,1)} all-reduce(f32[8,192,192]{2,1,0:T(8,128)} %reshape.31), channel_id=1, replica_groups=mesh['gx'=2,'gy'=4,'gz'=4] {'gz'}, use_global_device_ids=true, to_apply=%region_2.3 | all-reduce | flops 294912 | bytes 1769472 | tf_op jit(solution)/shard_map/psum | solution.py:46
  239.8 2.6 convolution_convert_fusion
  242.4 0.0 all-gather.3.cloned.1.call-update
  242.5 0.1 copy.24
  242.6 0.1 reshape.36
  242.7 6.3 %reshape.27 = bf16[32,192,192]{2,1,0:T(8,128)(2,1)} reshape(bf16[32,36864]{1,0:T(8,128)(2,1)} %param.10) | data formatting | bytes 4718592 | tf_op jit(solution)/shard_map/reshape | solution.py:16
  249.0 51.4 %all-gather.5.cloned.1.call-done = bf16[64,192,192]{2,1,0:T(8,128)(2,1)} async-done(((bf16[8,192,192]{2,1,0:T(8,128)(2,1)}), bf16[64,192,192]{2,1,0:T(8,128)(2,1)}) %all-gather.5.cloned.1.call-update) | async-done | bytes 4718608 | tf_op jit(solution)/shard_map/all_gather | solution.py:55
  300.4 6.3 %gather_fusion.1 = bf16[64,192,192]{2,1,0:T(8,128)(2,1)} fusion(bf16[64,192,192]{2,1,0:T(8,128)(2,1)} %all-gather.5.cloned.1.call-done, s32[1024]{0:T(1024)S(1)} %pad_clamp_fusion), kind=kCustom, calls=%fused_computation.1 | custom fusion | bytes 9437440 | tf_op jit(solution)/shard_map/gather | solution.py:57
  306.7 92.7 %all-gather.3.cloned.1.call-done = bf16[64,192,192]{2,1,0:T(8,128)(2,1)} async-done(((bf16[8,192,192]{2,1,0:T(8,128)(2,1)}), bf16[64,192,192]{2,1,0:T(8,128)(2,1)}) %all-gather.3.cloned.1.call-update) | async-done | bytes 4718608 | tf_op jit(solution)/shard_map/all_gather | solution.py:54
  399.4 6.4 %gather_fusion = bf16[64,192,192]{2,1,0:T(8,128)(2,1)} fusion(bf16[64,192,192]{2,1,0:T(8,128)(2,1)} %all-gather.3.cloned.1.call-done, s32[1024]{0:T(1024)S(1)} %pad_clamp_fusion), kind=kCustom, calls=%fused_computation | custom fusion | bytes 9437440 | tf_op jit(solution)/shard_map/gather | solution.py:58
  405.9 9.7 %copy.25 = f32[64,192,192]{1,2,0:T(8,128)} copy(bf16[64,192,192]{2,1,0:T(8,128)(2,1)} %gather_fusion) | data formatting | bytes 14155776 | tf_op jit(solution)/shard_map/convert_element_type | solution.py:62
  415.5 11.3 %fusion = bf16[32,2,192,192]{2,3,1,0:T(8,128)(2,1)} fusion(f32[32,2,192,192]{2,3,1,0:T(8,128)} %bitcast.27, bf16[32,2,192,192]{3,2,1,0:T(8,128)(2,1)} %bitcast.28, bf16[32,192,192]{2,1,0:T(8,128)(2,1)} %fusion.19), kind=kOutput, calls=%fused_computation.3 | convolution fusion | flops 915406848 | bytes 21233664 | tf_op jit(solution)/shard_map/pab,pebc->peac/dot_general | solution.py:59
  426.8 7.5 %fusion.9 = f32[32,192,192]{2,1,0:T(8,128)} fusion(bf16[32,192,192]{2,1,0:T(8,128)(2,1)S(1)} %reshape.29, bf16[32,2,192,192]{2,3,1,0:T(8,128)(2,1)} %fusion), kind=kOutput, calls=%fused_computation.15 | convolution fusion | flops 911867904 | bytes 15728640 | tf_op jit(solution)/shard_map/pab,pbc->pac/dot_general | solution.py:71
  434.3 7.9 %select_convert_fusion = bf16[32,192,192]{2,1,0:T(8,128)(2,1)S(1)} fusion(f32[32,192,192]{2,1,0:T(8,128)} %fusion.9, bf16[32,192,192]{2,1,0:T(8,128)(2,1)} %reshape.27, s32[32]{0:T(128)S(1)} %add_multiply_fusion, bf16[32,192,192]{2,1,0:T(8,128)(2,1)} %reshape.28), kind=kOutput, calls=%fused_computation.4 | convolution fusion | flops 467140608 | bytes 11796608 | tf_op jit(solution)/shard_map/pab,pbc->pac/dot_general | solution.py:34
  442.1 4.2 reshape.33
  (3 shorter events, 0.0 us)
Async XLA Ops:
  6.5 195.1 %reduce-scatter.2.cloned.1.call-start = ((), (), s32[]{:S(2)}) async-start(), calls=%async_computation.1 | async-start | bytes 10616832 | tf_op jit(solution)/shard_map/reduce_scatter | solution.py:40
  12.7 5.0 %copy-start.1 = (s32[32]{0:T(128)S(1)}, s32[32]{0:T(128)}, u32[]{:S(2)}) copy-start(s32[32]{0:T(128)} %param.7) | copy-start | bytes 388
  24.5 6.2 %copy-start = (s32[32,2]{0,1:T(2,128)S(1)}, s32[32,2]{0,1:T(2,128)}, u32[]{:S(2)}) copy-start(s32[32,2]{0,1:T(2,128)} %param.6) | copy-start | bytes 772
  37.5 262.9 %all-gather.5.cloned.1.call-start = ((), (), s32[]{:S(2)}) async-start(), calls=%async_computation.3 | async-start | bytes 7077888 | tf_op jit(solution)/shard_map/all_gather | solution.py:55
  40.5 359.0 %all-gather.3.cloned.1.call-start = ((), (), s32[]{:S(2)}) async-start(), calls=%async_computation.2 | async-start | bytes 7077888 | tf_op jit(solution)/shard_map/all_gather | solution.py:54
Sparse Core Ops, SparseCore 0:
  37.6 164.0 reduce-scatter.1
  203.8 96.5 all-gather.4
  302.5 96.8 all-gather.2
where the time goes:
time: 456 us; the launch traced here: 453 us
  waiting for transfers between devices  305 us (67%)
  local copies, waits for them, and re-layouts  56.4 us (12%)
  matrix products  42.8 us (9%)
  blocking collectives  35 us (8%)
  between operations  13.2 us (3%)
    reduce_scatter x1, waiting for transfers between devices, body(): lax.psum_scatter(jnp.dot(end_counts, flat_projected, preferred_element_ty...  161 us
    all_gather x1, waiting for transfers between devices, body(): lax.all_gather(coupled, ('gx', 'gy'), axis=0, tiled=True)  92.7 us
    all_gather x1, waiting for transfers between devices, body(): lax.all_gather(exchange_blocks, ('gx', 'gy'), axis=0, tiled=True)  51.4 us
    psum x1, blocking collectives, body(): domain = lax.psum(partial_sum, 'gz')  35 us
    dot_general x1, matrix products, body(): jnp.einsum('pab,pebc->peac', projected, picked_blocks, preferred_element_...  11.3 us
    convert_element_type x1, local copies, waits for them, and re-layouts, body(): picked_coupled.astype(jnp.float32) - own_term.astype(jnp.float32)  9.66 us
  transfers between devices with their start and end apart: 3, of which 3 were waited for; matrix products, arithmetic and copies ran while one was open for 5% of the time, Pallas kernels for 0%

commit v1 on v0

v1 whole, which is shorter than its diff:
```python
import functools

import jax
import jax.numpy as jnp
import numpy as np
from jax import lax
from jax.experimental import pallas as pl
from jax.experimental.pallas import tpu as pltpu
from jax.sharding import PartitionSpec as P

RSTEP = 64
R = 192
LANES = 128
PIECES = 2
AXES = ("gx", "gy", "gz")
MESH = pl.DeviceIdType.MESH
BF = jnp.bfloat16
F32 = jnp.float32


def bits_of(mesh_shape):
    found, stride = {}, 1
    for axis in reversed(AXES):
        size = mesh_shape[axis]
        found[axis] = [(axis, 1 << b, stride << b) for b in range(size.bit_length() - 1)]
        stride *= size
    return found


def orders_of(mesh_shape):
    b = bits_of(mesh_shape)
    first, rest = b["gz"][:1], b["gz"][1:]
    return (first + rest + b["gx"] + b["gy"], first + b["gx"] + rest + b["gy"])


def dot(a, b, dims=((1,), (0,))):
    return lax.dot_general(a, b, (dims, ((), ())), preferred_element_type=F32)


def kernel(
    orders, rank_ref, named_ref, where_ref, amp_ref, int_ref, itg_ref, xown_ref, out_ref,
    proj, acc, land, cbuf, xbuf, own, loc, turned, send_sem, recv_sem,
):
    pairs = amp_ref.shape[0]
    stages = len(orders[0])
    units = 1 << stages
    rows = R // PIECES

    def partner(bit):
        axis, stride, _ = bit
        c = lax.axis_index(axis)
        return {axis: c + stride * (1 - 2 * ((c // stride) % 2))}

    order_of = [h % 2 for h in range(PIECES)]
    bit_of = lambda h, s: orders[order_of[h]][s]
    half = lambda s: units >> (s + 1)

    barrier = pltpu.get_barrier_semaphore()
    for bit in orders[0]:
        pl.semaphore_signal(barrier, inc=1, device_id=partner(bit), device_id_type=MESH)
    pl.semaphore_wait(barrier, stages)

    def remote(kind, src, dst, h, s):
        return pltpu.make_async_remote_copy(
            src_ref=src, dst_ref=dst, send_sem=send_sem.at[kind, h, s], recv_sem=recv_sem.at[kind, h, s],
            device_id=partner(bit_of(h, s)), device_id_type=MESH,
        )

    def reduce_copy(h, s):
        n = half(s)
        return remote(0, acc.at[h, pl.ds(n, n)], land.at[h, pl.ds(n, n)], h, s)

    def gather_copy(kind, buf, h, s):
        n = half(s)
        return remote(kind, buf.at[h, pl.ds(0, n)], buf.at[h, pl.ds(n, n)], h, s)

    def pack(ref, h, j, a, b):
        ref[h, j, 0] = a[:, :LANES]
        ref[h, j, 1] = b[:, :LANES]
        ref[h, j, 2] = jnp.concatenate([a[:, LANES:], b[:, LANES:]], axis=1)

    for h in range(PIECES):
        span = pl.ds(h * rows, rows)
        pack(xbuf, h, 0, xown_ref[0, span], xown_ref[1, span])
    for h in range(PIECES):
        gather_copy(2, xbuf, h, stages - 1).start()

    def x_step(s):
        for h in range(PIECES):
            gather_copy(2, xbuf, h, s).wait_recv()
            if s:
                gather_copy(2, xbuf, h, s - 1).start()

    row = lax.broadcasted_iota(jnp.int32, (R, R), 0)
    col = lax.broadcasted_iota(jnp.int32, (R, R), 1)
    reach = jnp.maximum(row, col)

    def masked(p):
        size = (rank_ref[p] + 1) * RSTEP
        return jnp.where(reach < size, amp_ref[p].astype(F32), 0.0).astype(BF)

    def project(p, carry):
        side = int_ref[p]
        h1 = dot(side, masked(p)).astype(BF)
        proj[p] = dot(h1, side, ((1,), (1,))).astype(BF)
        return carry

    proj[pairs] = jnp.zeros((R, R), BF)
    cut = [pairs * i // stages for i in range(stages + 1)]
    waits = list(range(stages - 1, 0, -1))
    for i in range(stages):
        lax.fori_loop(cut[i], cut[i + 1], project, 0, unroll=2)
        if i < len(waits) - 1:
            x_step(waits[i])

    def build(h, j, carry):
        span = pl.ds(h * rows, rows)
        base = (order_of[h] * units + j) * 4
        a = proj[named_ref[base], span] + proj[named_ref[base + 1], span]
        b = proj[named_ref[base + 2], span] + proj[named_ref[base + 3], span]
        pack(acc, h, j, a, b)
        return carry

    for h in range(PIECES):
        lax.fori_loop(units // 2, units, functools.partial(build, h), 0)
        reduce_copy(h, 0).start()
    x_step(1)
    for h in range(PIECES):
        lax.fori_loop(0, units // 2, functools.partial(build, h), 0)

    def local(p, carry):
        block = itg_ref[p]
        loc[p] = dot(masked(p), block) + block.astype(F32)
        turned[p] = int_ref[p].T
        return carry

    def fetch(buf, p, e):
        base = (p * 2 + e) * 3
        odd = where_ref[base + 2]
        parts = []
        for h in range(PIECES):
            at = where_ref[base + order_of[h]]
            tail = buf[h, at, 2]
            tail = jnp.where(odd == 1, tail[:, LANES // 2 :], tail[:, : LANES // 2])
            parts.append(jnp.concatenate([buf[h, at, odd], tail], axis=1))
        return jnp.concatenate(parts, axis=0)

    def own_part(p, carry):
        both = fetch(xbuf, p, 0) + fetch(xbuf, p, 1)
        own[p] = dot(proj[p], both).astype(BF)
        return carry

    def add(h, n, j, carry):
        acc[h, j] = acc[h, j] + land[h, n + j]
        return carry

    def reduce_step(s):
        n = half(s)
        for h in range(PIECES):
            reduce_copy(h, s).wait_recv()
            lax.fori_loop(n // 2, n, functools.partial(add, h, n), 0)
            if s + 1 < stages:
                reduce_copy(h, s + 1).start()
        for h in range(PIECES):
            lax.fori_loop(0, n // 2, functools.partial(add, h, n), 0)

    quarter = pairs // 4
    reduce_step(0)
    lax.fori_loop(0, pairs, local, 0, unroll=2)
    reduce_step(1)
    x_step(0)
    lax.fori_loop(0, 2 * quarter, own_part, 0, unroll=2)
    reduce_step(2)
    lax.fori_loop(2 * quarter, 3 * quarter, own_part, 0, unroll=2)
    for s in range(3, stages):
        reduce_step(s)

    for h in range(PIECES):
        left = [acc[h, 0, t] for t in range(2)]
        tail = acc[h, 0, 2]
        done = []
        for t in range(2):
            block = jnp.concatenate([left[t], tail[:, t * (LANES // 2) : (t + 1) * (LANES // 2)]], axis=1)
            done.append(dot(block, xown_ref[t]).astype(BF))
        pack(cbuf, h, 0, *done)
        gather_copy(1, cbuf, h, stages - 1).start()
    lax.fori_loop(3 * quarter, pairs, own_part, 0, unroll=2)
    for s in range(stages - 1, -1, -1):
        for h in range(PIECES):
            gather_copy(1, cbuf, h, s).wait_recv()
            if s:
                gather_copy(1, cbuf, h, s - 1).start()

    def finish(p, carry):
        total = fetch(cbuf, p, 0).astype(F32) + fetch(cbuf, p, 1).astype(F32) - own[p].astype(F32)
        half_back = dot(turned[p], total.astype(BF)).astype(BF)
        result = loc[p] + dot(half_back, int_ref[p])
        size = (rank_ref[p] + 1) * RSTEP
        out_ref[p] = jnp.where(reach < size, result, 0.0).astype(BF)
        return carry

    lax.fori_loop(0, pairs, finish, 0, unroll=2)

    for h in range(PIECES):
        for s in range(stages):
            reduce_copy(h, s).wait_send()
            gather_copy(1, cbuf, h, s).wait_send()
            gather_copy(2, xbuf, h, s).wait_send()


def fused(orders, pair_list, rank_bucket, amplitudes, intersects, integrals, exchange_blocks):
    pairs = amplitudes.shape[0]
    stages = len(orders[0])
    units = 1 << stages
    me = jnp.int32(0)
    for axis in AXES:
        me = me * lax.axis_size(axis) + lax.axis_index(axis)

    named, where = [], []
    unit_of_end = pair_list // 2
    for order in orders:
        at = np.arange(units)
        relative = sum(((at >> (stages - 1 - s)) & 1) * order[s][2] for s in range(stages))
        orbital = 2 * (jnp.asarray(relative, jnp.int32) ^ me)[:, None] + jnp.arange(2, dtype=jnp.int32)[None]
        hit = jnp.any(pair_list[None, None] == orbital[:, :, None, None], axis=3)
        spot = jnp.arange(pairs, dtype=jnp.int32)
        first = jnp.min(jnp.where(hit, spot, pairs), axis=2)
        last = jnp.max(jnp.where(hit, spot, -1), axis=2)
        last = jnp.where(last > first, last, pairs)
        named.append(jnp.stack([first, last], axis=2).reshape(-1))
        apart = unit_of_end ^ me
        where.append(sum(((apart // order[s][2]) % 2) << (stages - 1 - s) for s in range(stages)))
    where.append(pair_list % 2)
    named = jnp.concatenate(named)
    where = jnp.stack(where, axis=2).reshape(-1)

    square = lambda a: a.reshape(a.shape[0], R, R)
    mine = lax.dynamic_slice_in_dim(exchange_blocks, lax.axis_index("gz") * 2, 2, 0)
    rows = R // PIECES
    whole = (PIECES, units, 3, rows, LANES)
    smem = pl.BlockSpec(memory_space=pltpu.SMEM)
    vmem = pl.BlockSpec(memory_space=pltpu.VMEM)
    result = pl.pallas_call(
        functools.partial(kernel, orders),
        out_shape=jax.ShapeDtypeStruct((pairs, R, R), BF),
        in_specs=[smem] * 3 + [vmem] * 4,
        out_specs=vmem,
        scratch_shapes=[
            pltpu.VMEM((pairs + 1, R, R), BF),
            pltpu.VMEM(whole, BF),
            pltpu.VMEM(whole, BF),
            pltpu.VMEM(whole, BF),
            pltpu.VMEM(whole, BF),
            pltpu.VMEM((pairs, R, R), BF),
            pltpu.VMEM((pairs, R, R), F32),
            pltpu.VMEM((pairs, R, R), BF),
            pltpu.SemaphoreType.DMA((3, PIECES, stages)),
            pltpu.SemaphoreType.DMA((3, PIECES, stages)),
        ],
        compiler_params=pltpu.CompilerParams(
            collective_id=0, has_side_effects=True, vmem_limit_bytes=60 * 1024 * 1024
        ),
    )(rank_bucket, named, where, square(amplitudes), square(intersects), square(integrals), square(mine))
    return result.reshape(pairs, R * R)


def plain(pair_list, rank_bucket, amplitudes, intersects, integrals, exchange_blocks):
    pair_rows, owned_rows = amplitudes.shape[0], exchange_blocks.shape[0]
    square = lambda a: a.reshape(a.shape[0], R, R)
    amplitudes, intersects, integrals = map(square, (amplitudes, intersects, integrals))
    exchange_blocks = square(exchange_blocks)
    occupied = owned_rows * lax.axis_size("gx") * lax.axis_size("gy")
    reach = jnp.maximum(lax.broadcasted_iota(jnp.int32, (R, R), 0), lax.broadcasted_iota(jnp.int32, (R, R), 1))
    inside = reach[None] < ((rank_bucket + 1) * RSTEP)[:, None, None]
    ein = functools.partial(jnp.einsum, preferred_element_type=F32)
    masked = jnp.where(inside, amplitudes, jnp.zeros_like(amplitudes))
    half_projected = ein("pab,pbc->pac", intersects, masked).astype(BF)
    projected = ein("pab,pcb->pac", half_projected, intersects).astype(BF)
    local_term = ein("pab,pbc->pac", masked, integrals)
    counts = jnp.sum(
        (pair_list[None] == lax.broadcasted_iota(jnp.int32, (occupied, 1, 1), 0)).astype(jnp.int32), axis=2
    ).astype(BF)
    share = jnp.dot(counts, projected.reshape(pair_rows, R * R), preferred_element_type=F32)
    share = lax.psum_scatter(share, ("gx", "gy"), scatter_dimension=0, tiled=True)
    domain = lax.psum(share.reshape(owned_rows, R, R), "gz")
    coupled = ein("oab,obc->oac", domain.astype(BF), exchange_blocks).astype(BF)
    every_coupled = lax.all_gather(coupled, ("gx", "gy"), axis=0, tiled=True)
    every_block = lax.all_gather(exchange_blocks, ("gx", "gy"), axis=0, tiled=True)
    own_term = ein("pab,pebc->peac", projected, every_block[pair_list]).astype(BF)
    answers = (every_coupled[pair_list].astype(F32) - own_term.astype(F32)).astype(BF)
    combined = (answers[:, 0].astype(F32) + answers[:, 1].astype(F32)).astype(BF)
    half_back = ein("pba,pbc->pac", intersects, combined).astype(BF)
    total = integrals.astype(F32) + local_term + ein("pab,pbc->pac", half_back, intersects)
    return jnp.where(inside, total, jnp.zeros_like(total)).astype(BF).reshape(pair_rows, R * R)


def solution(mesh):
    shape = dict(mesh.shape)
    split = P(AXES, None)
    powers = all(shape[a] & (shape[a] - 1) == 0 for a in AXES) and shape["gz"] > 1

    def body(*args):
        if powers and args[5].shape[0] == 2 * shape["gz"]:
            return fused(orders_of(shape), *args)
        return plain(*args)

    return jax.shard_map(
        body, mesh=mesh, in_specs=(split, P(AXES), split, split, split, P(("gx", "gy"), None)),
        out_specs=split, check_vma=False,
    )
```

time: 456 us -> 153 us (0.34)
  the two profiles are of different devices: /device:TPU:1 before, /device:TPU:13 now
where the time goes in v1:
time: 153 us; the launch traced here: 152 us
  Pallas kernels  123 us (80%)
  local copies, waits for them, and re-layouts  25.5 us (17%)
  other arithmetic  3.85 us (3%)
    pallas_call x1, Pallas kernels, fused(): pl.pallas_call(functools.partial(kernel, orders), out_shape=jax.ShapeDtyp...  123 us
    reshape x4, local copies, waits for them, and re-layouts, fused(): square = lambda a: a.reshape(a.shape[0], R, R)  17.8 us
    reshape x1, local copies, waits for them, and re-layouts, fused(): return result.reshape(pairs, R * R)  6.18 us

profile of v1, /device:TPU:13, one launch (start us, length us, event | category | flops | bytes accessed | tf_op | source)
XLA Modules:
  0.0 152.2 jit_solution(9580445504002865272)
XLA Ops:
  0.0 0.0 copy-start
  0.0 0.7 xor_multiply_fusion
  0.8 0.7 sign_compare_fusion
  1.5 0.7 fusion.3
  2.2 0.8 compare_reduce_fusion.1
  3.0 0.1 select_reduce_fusion.3
  3.1 0.1 select_reduce_fusion.1
  3.3 0.1 copy.18
  3.4 0.7 reshape.99.where_ref
  4.1 0.0 copy-start.1
  4.1 0.1 copy.17
  4.2 0.1 reshape.98
  4.4 0.1 copy.16
  4.5 0.2 reshape.97
  4.7 0.6 pad_add_fusion.3.named_ref
  5.2 0.0 copy-done
  5.2 0.2 constant_dynamic-slice_fusion
  5.4 0.9 reshape.103.xown_ref
  6.3 6.1 %reshape.100.amp_ref = bf16[32,192,192]{2,1,0:T(8,128)(2,1)} reshape(bf16[32,36864]{1,0:T(8,128)(2,1)} %param.10) | data formatting | bytes 4718592 | tf_op jit(solution)/shard_map/reshape | solution.py:237
  12.4 0.0 copy-done.1
  12.4 4.6 %reshape.101.int_ref = bf16[32,192,192]{2,1,0:T(8,128)(2,1)} reshape(bf16[32,36864]{1,0:T(8,128)(2,1)S(1)} %copy-done.1) | data formatting | bytes 4718592 | tf_op jit(solution)/shard_map/reshape | solution.py:237
  17.0 6.2 %reshape.102.itg_ref = bf16[32,192,192]{2,1,0:T(8,128)(2,1)} reshape(bf16[32,36864]{1,0:T(8,128)(2,1)} %param.12) | data formatting | bytes 4718592 | tf_op jit(solution)/shard_map/reshape | solution.py:237
  23.2 122.8 %shard_map.82 = bf16[32,192,192]{2,1,0:T(8,128)(2,1)} custom-call(s32[32]{0:T(128)} %rank_ref.1, s32[256]{0:T(256)} %pad_add_fusion.3.named_ref, s32[192]{0:T(256)} %reshape.99.where_ref, bf16[32,192,192]{2,1,0:T(8,128)(2,1)} %reshape.100.amp_ref, bf16[32,192,192]{2,1,0:T(8,128)(2,1)} %reshape.101.int_ref, bf16[32,192,192]{2,1,0:T(8,128)(2,1)} %reshape.102.itg_ref, ...), custom_call_target="tpu_custom_call" | custom-call | tf_op jit(solution)/shard_map/pallas_call | solution.py:243
  146.1 6.2 %reshape.104 = bf16[32,36864]{1,0:T(8,128)(2,1)} reshape(bf16[32,192,192]{2,1,0:T(8,128)(2,1)} %shard_map.82) | data formatting | bytes 4718592 | tf_op jit(solution)/shard_map/reshape | solution.py:264
  (8 shorter events, 0.1 us)
Async XLA Ops:
  0.0 5.2 %copy-start = (bf16[8,36864]{1,0:T(8,128)(2,1)S(1)}, bf16[8,36864]{1,0:T(8,128)(2,1)}, u32[]{:S(2)}) copy-start(bf16[8,36864]{1,0:T(8,128)(2,1)} %param.13) | copy-start | bytes 1769476
  4.1 8.3 %copy-start.1 = (bf16[32,36864]{1,0:T(8,128)(2,1)S(1)}, bf16[32,36864]{1,0:T(8,128)(2,1)}, u32[]{:S(2)}) copy-start(bf16[32,36864]{1,0:T(8,128)(2,1)} %param.11) | copy-start | bytes 7077892

commit v2 on v1

--- a/solution.py
+++ b/solution.py
@@ -11,7 +11,9 @@
 RSTEP = 64
 R = 192
 LANES = 128
-PIECES = 2
+PIECES = 4
+LAG = 1
+X3, X2, X1, X0 = 1, 2, 4, 7
 AXES = ("gx", "gy", "gz")
 MESH = pl.DeviceIdType.MESH
 BF = jnp.bfloat16
@@ -38,10 +40,10 @@
 
 
 def kernel(
-    orders, rank_ref, named_ref, where_ref, amp_ref, int_ref, itg_ref, xown_ref, out_ref,
-    proj, acc, land, cbuf, xbuf, own, loc, turned, send_sem, recv_sem,
+    orders, rank_ref, named_ref, where_ref, amp_raw, int_raw, itg_raw, xown_raw, out_ref,
+    amp_ref, int_ref, itg_ref, xown_ref, proj, acc, land, cbuf, xbuf, own, loc, turned, send_sem, recv_sem,
 ):
-    pairs = amp_ref.shape[0]
+    pairs = amp_raw.shape[0]
     stages = len(orders[0])
     units = 1 << stages
     rows = R // PIECES
@@ -79,6 +81,16 @@
         ref[h, j, 1] = b[:, :LANES]
         ref[h, j, 2] = jnp.concatenate([a[:, LANES:], b[:, LANES:]], axis=1)
 
+    row = lax.broadcasted_iota(jnp.int32, (R, R), 0)
+    col = lax.broadcasted_iota(jnp.int32, (R, R), 1)
+    natural = jnp.where(row < R // 2, 2 * row, 2 * row - (R - 1))
+    reach = jnp.maximum(natural, col)
+    sort = (natural == col).astype(F32).astype(BF)
+
+    unsort = (lax.broadcasted_iota(jnp.int32, (R, R), 0) == jnp.where(col < R // 2, 2 * col, 2 * col - (R - 1))).astype(F32).astype(BF)
+
+    for t in range(2):
+        xown_ref[t] = dot(dot(sort, xown_raw[t]).astype(BF), sort, ((1,), (1,))).astype(BF)
     for h in range(PIECES):
         span = pl.ds(h * rows, rows)
         pack(xbuf, h, 0, xown_ref[0, span], xown_ref[1, span])
@@ -91,9 +103,18 @@
             if s:
                 gather_copy(2, xbuf, h, s - 1).start()
 
-    row = lax.broadcasted_iota(jnp.int32, (R, R), 0)
-    col = lax.broadcasted_iota(jnp.int32, (R, R), 1)
-    reach = jnp.maximum(row, col)
+    def relayout(raw, ref):
+        def some(c, carry):
+            at = pl.multiple_of(c * 16 * 2 * R, LANES)
+            top = pl.multiple_of(c * 16, 16)
+            low = pl.multiple_of(R // 2 + c * 16, 16)
+            for g in range(0, pairs, 16):
+                value = raw[g : g + 16, pl.ds(at, 16 * 2 * R)].reshape(16, 16, 2 * R)
+                ref[pl.ds(g, 16), pl.ds(top, 16), :] = value[:, :, :R]
+                ref[pl.ds(g, 16), pl.ds(low, 16), :] = value[:, :, R:]
+            return carry
+
+        lax.fori_loop(0, R // 32, some, 0)
 
     def masked(p):
         size = (rank_ref[p] + 1) * RSTEP
@@ -101,17 +122,17 @@
 
     def project(p, carry):
         side = int_ref[p]
-        h1 = dot(side, masked(p)).astype(BF)
+        middle = dot(unsort, masked(p)).astype(BF)
+        h1 = dot(side, middle).astype(BF)
         proj[p] = dot(h1, side, ((1,), (1,))).astype(BF)
         return carry
 
     proj[pairs] = jnp.zeros((R, R), BF)
-    cut = [pairs * i // stages for i in range(stages + 1)]
-    waits = list(range(stages - 1, 0, -1))
-    for i in range(stages):
-        lax.fori_loop(cut[i], cut[i + 1], project, 0, unroll=2)
-        if i < len(waits) - 1:
-            x_step(waits[i])
+    relayout(amp_raw, amp_ref)
+    relayout(int_raw, int_ref)
+    lax.fori_loop(0, pairs // 2, project, 0, unroll=2)
+    x_step(stages - 1)
+    lax.fori_loop(pairs // 2, pairs, project, 0, unroll=2)
 
     def build(h, j, carry):
         span = pl.ds(h * rows, rows)
@@ -124,14 +145,14 @@
     for h in range(PIECES):
         lax.fori_loop(units // 2, units, functools.partial(build, h), 0)
         reduce_copy(h, 0).start()
-    x_step(1)
     for h in range(PIECES):
         lax.fori_loop(0, units // 2, functools.partial(build, h), 0)
 
     def local(p, carry):
         block = itg_ref[p]
-        loc[p] = dot(masked(p), block) + block.astype(F32)
-        turned[p] = int_ref[p].T
+        middle = dot(unsort, block).astype(BF)
+        loc[p] = dot(masked(p), middle) + block.astype(F32)
+        turned[p] = dot(sort, int_ref[p], ((1,), (1,))).astype(BF)
         return carry
 
     def fetch(buf, p, e):
@@ -154,49 +175,56 @@
         acc[h, j] = acc[h, j] + land[h, n + j]
         return carry
 
-    def reduce_step(s):
-        n = half(s)
-        for h in range(PIECES):
-            reduce_copy(h, s).wait_recv()
-            lax.fori_loop(n // 2, n, functools.partial(add, h, n), 0)
-            if s + 1 < stages:
-                reduce_copy(h, s + 1).start()
-        for h in range(PIECES):
-            lax.fori_loop(0, n // 2, functools.partial(add, h, n), 0)
-
-    quarter = pairs // 4
-    reduce_step(0)
-    lax.fori_loop(0, pairs, local, 0, unroll=2)
-    reduce_step(1)
-    x_step(0)
-    lax.fori_loop(0, 2 * quarter, own_part, 0, unroll=2)
-    reduce_step(2)
-    lax.fori_loop(2 * quarter, 3 * quarter, own_part, 0, unroll=2)
-    for s in range(3, stages):
-        reduce_step(s)
-
-    for h in range(PIECES):
-        left = [acc[h, 0, t] for t in range(2)]
+    def couple(h):
         tail = acc[h, 0, 2]
         done = []
         for t in range(2):
-            block = jnp.concatenate([left[t], tail[:, t * (LANES // 2) : (t + 1) * (LANES // 2)]], axis=1)
+            block = jnp.concatenate([acc[h, 0, t], tail[:, t * (LANES // 2) : (t + 1) * (LANES // 2)]], axis=1)
             done.append(dot(block, xown_ref[t]).astype(BF))
         pack(cbuf, h, 0, *done)
         gather_copy(1, cbuf, h, stages - 1).start()
-    lax.fori_loop(3 * quarter, pairs, own_part, 0, unroll=2)
-    for s in range(stages - 1, -1, -1):
-        for h in range(PIECES):
+
+    def advance(h, step):
+        if step >= stages:
+            s = 2 * stages - 1 - step
             gather_copy(1, cbuf, h, s).wait_recv()
             if s:
                 gather_copy(1, cbuf, h, s - 1).start()
+            return
+        n = half(step)
+        reduce_copy(h, step).wait_recv()
+        lax.fori_loop(n // 2, n, functools.partial(add, h, n), 0)
+        if step + 1 < stages:
+            reduce_copy(h, step + 1).start()
+        lax.fori_loop(0, n // 2, functools.partial(add, h, n), 0)
+        if step + 1 == stages:
+            couple(h)
+
+    groups = PIECES // 2
+    last = groups - 1
+    after = {
+        (0, 0): [lambda: relayout(itg_raw, itg_ref), lambda: lax.fori_loop(0, pairs, local, 0, unroll=2)],
+        (last, X3): [lambda: x_step(3)],
+        (last, X2): [lambda: x_step(2)],
+        (last, X1): [lambda: x_step(1)],
+        (last, X0): [lambda: x_step(0), lambda: lax.fori_loop(0, pairs, own_part, 0, unroll=2)],
+    }
+    for time in range(2 * stages + LAG * last):
+        for group in range(groups):
+            step = time - LAG * group
+            if 0 <= step < 2 * stages:
+                for h in (2 * group, 2 * group + 1):
+                    advance(h, step)
+                for work in after.get((group, step), []):
+                    work()
 
     def finish(p, carry):
         total = fetch(cbuf, p, 0).astype(F32) + fetch(cbuf, p, 1).astype(F32) - own[p].astype(F32)
         half_back = dot(turned[p], total.astype(BF)).astype(BF)
         result = loc[p] + dot(half_back, int_ref[p])
         size = (rank_ref[p] + 1) * RSTEP
-        out_ref[p] = jnp.where(reach < size, result, 0.0).astype(BF)
+        result = jnp.where(reach < size, result, 0.0).astype(BF)
+        out_ref[p] = jnp.concatenate([result[: R // 2], result[R // 2 :]], axis=1)
         return carry
 
     lax.fori_loop(0, pairs, finish, 0, unroll=2)
@@ -208,44 +236,71 @@
             gather_copy(2, xbuf, h, s).wait_send()
 
 
-def fused(orders, pair_list, rank_bucket, amplitudes, intersects, integrals, exchange_blocks):
-    pairs = amplitudes.shape[0]
+def tables(orders, list_ref, named_ref, where_ref):
+    pairs = list_ref.shape[0]
     stages = len(orders[0])
     units = 1 << stages
     me = jnp.int32(0)
     for axis in AXES:
         me = me * lax.axis_size(axis) + lax.axis_index(axis)
 
-    named, where = [], []
-    unit_of_end = pair_list // 2
-    for order in orders:
-        at = np.arange(units)
-        relative = sum(((at >> (stages - 1 - s)) & 1) * order[s][2] for s in range(stages))
-        orbital = 2 * (jnp.asarray(relative, jnp.int32) ^ me)[:, None] + jnp.arange(2, dtype=jnp.int32)[None]
-        hit = jnp.any(pair_list[None, None] == orbital[:, :, None, None], axis=3)
-        spot = jnp.arange(pairs, dtype=jnp.int32)
-        first = jnp.min(jnp.where(hit, spot, pairs), axis=2)
-        last = jnp.max(jnp.where(hit, spot, -1), axis=2)
-        last = jnp.where(last > first, last, pairs)
-        named.append(jnp.stack([first, last], axis=2).reshape(-1))
-        apart = unit_of_end ^ me
-        where.append(sum(((apart // order[s][2]) % 2) << (stages - 1 - s) for s in range(stages)))
-    where.append(pair_list % 2)
-    named = jnp.concatenate(named)
-    where = jnp.stack(where, axis=2).reshape(-1)
+    def clear(i, carry):
+        for b in range(8):
+            named_ref[i * 8 + b] = pairs
+        return carry
+
+    lax.fori_loop(0, units, clear, 0)
+
+    def put(p, carry):
+        for e in range(2):
+            orbital = list_ref[p, e]
+            apart = (orbital >> 1) ^ me
+            odd = orbital & 1
+            base = (p * 2 + e) * 3
+            for o, order in enumerate(orders):
+                place = jnp.int32(0)
+                for bit in order:
+                    place = place * 2 + ((apart >> (bit[2].bit_length() - 1)) & 1)
+                where_ref[base + o] = place
+                slot = (o * units + place) * 4 + odd * 2
+                slot = jnp.where(named_ref[slot] == pairs, slot, slot + 1)
+                named_ref[slot] = p
+            where_ref[base + 2] = odd
+        return carry
+
+    lax.fori_loop(0, pairs, put, 0)
+
+
+def fused(orders, pair_list, rank_bucket, amplitudes, intersects, integrals, exchange_blocks):
+    pairs = amplitudes.shape[0]
+    stages = len(orders[0])
+    units = 1 << stages
+    smem = pl.BlockSpec(memory_space=pltpu.SMEM)
+    named, where = pl.pallas_call(
+        functools.partial(tables, orders),
+        out_shape=(
+            jax.ShapeDtypeStruct((2 * units * 4,), jnp.int32),
+            jax.ShapeDtypeStruct((pairs * 2 * 3,), jnp.int32),
+        ),
+        in_specs=[smem],
+        out_specs=(smem, smem),
+    )(pair_list)
 
     square = lambda a: a.reshape(a.shape[0], R, R)
     mine = lax.dynamic_slice_in_dim(exchange_blocks, lax.axis_index("gz") * 2, 2, 0)
     rows = R // PIECES
     whole = (PIECES, units, 3, rows, LANES)
-    smem = pl.BlockSpec(memory_space=pltpu.SMEM)
     vmem = pl.BlockSpec(memory_space=pltpu.VMEM)
     result = pl.pallas_call(
         functools.partial(kernel, orders),
-        out_shape=jax.ShapeDtypeStruct((pairs, R, R), BF),
+        out_shape=jax.ShapeDtypeStruct((pairs, R // 2, 2 * R), BF),
         in_specs=[smem] * 3 + [vmem] * 4,
         out_specs=vmem,
         scratch_shapes=[
+            pltpu.VMEM((pairs, R, R), BF),
+            pltpu.VMEM((pairs, R, R), BF),
+            pltpu.VMEM((pairs, R, R), BF),
+            pltpu.VMEM((2, R, R), BF),
             pltpu.VMEM((pairs + 1, R, R), BF),
             pltpu.VMEM(whole, BF),
             pltpu.VMEM(whole, BF),
@@ -260,7 +315,7 @@
         compiler_params=pltpu.CompilerParams(
             collective_id=0, has_side_effects=True, vmem_limit_bytes=60 * 1024 * 1024
         ),
-    )(rank_bucket, named, where, square(amplitudes), square(intersects), square(integrals), square(mine))
+    )(rank_bucket, named, where, amplitudes, intersects, integrals, square(mine))
     return result.reshape(pairs, R * R)
 
 

time: 153 us -> 125 us (0.82)
  the two profiles are of different devices: /device:TPU:13 before, /device:TPU:1 now
where the time goes in v2:
time: 125 us; the launch traced here: 124 us
  Pallas kernels  118 us (94%)
  local copies, waits for them, and re-layouts  6.42 us (5%)
    pallas_call x1, Pallas kernels, fused(): pl.pallas_call(functools.partial(kernel, orders), out_shape=jax.ShapeDtyp...  115 us
    unnamed x4, local copies, waits for them, and re-layouts  5.37 us
    pallas_call x1, Pallas kernels, fused(): pl.pallas_call(functools.partial(tables, orders), out_shape=(jax.ShapeDty...  3.12 us

profile of v2, /device:TPU:1, one launch (start us, length us, event | category | flops | bytes accessed | tf_op | source)
XLA Modules:
  0.0 124.4 jit_solution(4379836856945634579)
XLA Ops:
  0.0 0.0 copy-start
  0.0 1.4 %copy.7.list_ref = s32[32,2]{1,0:T(8,128)} copy(s32[32,2]{0,1:T(2,128)} %param.6) | data formatting | bytes 512 | tf_op args[0]
  1.4 3.1 %shard_map.64 = (s32[256]{0:T(256)}, s32[192]{0:T(256)}) custom-call(s32[32,2]{1,0:T(8,128)} %copy.7.list_ref), custom_call_target="tpu_custom_call" | custom-call | tf_op jit(solution)/shard_map/pallas_call | solution.py:279
  4.6 0.0 copy-done
  4.6 0.2 constant_dynamic-slice_fusion
  4.7 0.9 reshape.6.xown_raw
  5.6 114.8 %shard_map.65 = bf16[32,96,384]{2,1,0:T(8,128)(2,1)} custom-call(s32[32]{0:T(128)} %rank_ref.1, s32[256]{0:T(256)} %get-tuple-element.7.named_ref, s32[192]{0:T(256)} %get-tuple-element.8.where_ref, bf16[32,36864]{1,0:T(8,128)(2,1)} %amp_raw.1, bf16[32,36864]{1,0:T(8,128)(2,1)} %int_raw.1, bf16[32,36864]{1,0:T(8,128)(2,1)} %itg_raw.1, ...), custom_call_target="tpu_custom_call" | custom-call | tf_op jit(solution)/shard_map/pallas_call | solution.py:294
  120.4 3.9 %copy.8 = bf16[4,8,96,384]{3,1,2,0:T(8,128)(2,1)} copy(bf16[4,8,96,384]{3,2,1,0:T(8,128)(2,1)} %bitcast.2) | data formatting | bytes 4718592
Async XLA Ops:
  0.0 4.6 %copy-start = (bf16[8,36864]{1,0:T(8,128)(2,1)S(1)}, bf16[8,36864]{1,0:T(8,128)(2,1)}, u32[]{:S(2)}) copy-start(bf16[8,36864]{1,0:T(8,128)(2,1)} %param.11) | copy-start | bytes 1769476

commit v3 on v2

--- a/solution.py
+++ b/solution.py
@@ -13,7 +13,7 @@
 LANES = 128
 PIECES = 4
 LAG = 1
-X3, X2, X1, X0 = 1, 2, 4, 7
+X2, X1, X0 = 2, 5, 7
 AXES = ("gx", "gy", "gz")
 MESH = pl.DeviceIdType.MESH
 BF = jnp.bfloat16
@@ -130,9 +130,10 @@
     proj[pairs] = jnp.zeros((R, R), BF)
     relayout(amp_raw, amp_ref)
     relayout(int_raw, int_ref)
-    lax.fori_loop(0, pairs // 2, project, 0, unroll=2)
+    lax.fori_loop(0, pairs // 2, project, 0, unroll=8)
     x_step(stages - 1)
-    lax.fori_loop(pairs // 2, pairs, project, 0, unroll=2)
+    lax.fori_loop(pairs // 2, pairs, project, 0, unroll=8)
+    x_step(3)
 
     def build(h, j, carry):
         span = pl.ds(h * rows, rows)
@@ -143,10 +144,10 @@
         return carry
 
     for h in range(PIECES):
-        lax.fori_loop(units // 2, units, functools.partial(build, h), 0)
+        lax.fori_loop(units // 2, units, functools.partial(build, h), 0, unroll=8)
         reduce_copy(h, 0).start()
     for h in range(PIECES):
-        lax.fori_loop(0, units // 2, functools.partial(build, h), 0)
+        lax.fori_loop(0, units // 2, functools.partial(build, h), 0, unroll=8)
 
     def local(p, carry):
         block = itg_ref[p]
@@ -193,21 +194,21 @@
             return
         n = half(step)
         reduce_copy(h, step).wait_recv()
-        lax.fori_loop(n // 2, n, functools.partial(add, h, n), 0)
+        lax.fori_loop(n // 2, n, functools.partial(add, h, n), 0, unroll=True if n <= 4 else 4)
         if step + 1 < stages:
             reduce_copy(h, step + 1).start()
-        lax.fori_loop(0, n // 2, functools.partial(add, h, n), 0)
+        lax.fori_loop(0, n // 2, functools.partial(add, h, n), 0, unroll=True if n <= 4 else 4)
         if step + 1 == stages:
             couple(h)
 
     groups = PIECES // 2
     last = groups - 1
     after = {
-        (0, 0): [lambda: relayout(itg_raw, itg_ref), lambda: lax.fori_loop(0, pairs, local, 0, unroll=2)],
-        (last, X3): [lambda: x_step(3)],
+        (0, 0): [lambda: relayout(itg_raw, itg_ref), lambda: lax.fori_loop(0, pairs, local, 0, unroll=4)],
+
         (last, X2): [lambda: x_step(2)],
         (last, X1): [lambda: x_step(1)],
-        (last, X0): [lambda: x_step(0), lambda: lax.fori_loop(0, pairs, own_part, 0, unroll=2)],
+        (last, X0): [lambda: x_step(0), lambda: lax.fori_loop(0, pairs, own_part, 0, unroll=4)],
     }
     for time in range(2 * stages + LAG * last):
         for group in range(groups):
@@ -227,7 +228,7 @@
         out_ref[p] = jnp.concatenate([result[: R // 2], result[R // 2 :]], axis=1)
         return carry
 
-    lax.fori_loop(0, pairs, finish, 0, unroll=2)
+    lax.fori_loop(0, pairs, finish, 0, unroll=8)
 
     for h in range(PIECES):
         for s in range(stages):

time: 125 us -> 107 us (0.86)
  Pallas kernels: 118 us -> 101 us
    pallas_call x1, Pallas kernels: 115 us -> 97.5 us  [fused(): pl.pallas_call(functools.partial(kernel, orders), out_shape=jax.ShapeDtyp...]
where the time goes in v3:
time: 107 us
  Pallas kernels  101 us (94%)
  local copies, waits for them, and re-layouts  6.42 us (6%)
    pallas_call x1, Pallas kernels, fused(): pl.pallas_call(functools.partial(kernel, orders), out_shape=jax.ShapeDtyp...  97.5 us
    unnamed x4, local copies, waits for them, and re-layouts  5.37 us
    pallas_call x1, Pallas kernels, fused(): pl.pallas_call(functools.partial(tables, orders), out_shape=(jax.ShapeDty...  3.12 us

profile of v3, /device:TPU:1, one launch (start us, length us, event | category | flops | bytes accessed | tf_op | source)
XLA Modules:
  0.0 107.1 jit_solution(2918996598692335623)
XLA Ops:
  0.0 0.0 copy-start
  0.0 1.4 %copy.7.list_ref = s32[32,2]{1,0:T(8,128)} copy(s32[32,2]{0,1:T(2,128)} %param.6) | data formatting | bytes 512 | tf_op args[0]
  1.4 3.1 %shard_map.64 = (s32[256]{0:T(256)}, s32[192]{0:T(256)}) custom-call(s32[32,2]{1,0:T(8,128)} %copy.7.list_ref), custom_call_target="tpu_custom_call" | custom-call | tf_op jit(solution)/shard_map/pallas_call | solution.py:280
  4.6 0.0 copy-done
  4.6 0.2 constant_dynamic-slice_fusion
  4.7 0.9 reshape.6.xown_raw
  5.6 97.5 %shard_map.65 = bf16[32,96,384]{2,1,0:T(8,128)(2,1)} custom-call(s32[32]{0:T(128)} %rank_ref.1, s32[256]{0:T(256)} %get-tuple-element.7.named_ref, s32[192]{0:T(256)} %get-tuple-element.8.where_ref, bf16[32,36864]{1,0:T(8,128)(2,1)} %amp_raw.1, bf16[32,36864]{1,0:T(8,128)(2,1)} %int_raw.1, bf16[32,36864]{1,0:T(8,128)(2,1)} %itg_raw.1, ...), custom_call_target="tpu_custom_call" | custom-call | tf_op jit(solution)/shard_map/pallas_call | solution.py:295
  103.1 3.9 %copy.8 = bf16[4,8,96,384]{3,1,2,0:T(8,128)(2,1)} copy(bf16[4,8,96,384]{3,2,1,0:T(8,128)(2,1)} %bitcast.2) | data formatting | bytes 4718592
Async XLA Ops:
  0.0 4.6 %copy-start = (bf16[8,36864]{1,0:T(8,128)(2,1)S(1)}, bf16[8,36864]{1,0:T(8,128)(2,1)}, u32[]{:S(2)}) copy-start(bf16[8,36864]{1,0:T(8,128)(2,1)} %param.11) | copy-start | bytes 1769476
